TPU v7x, 256 devices: a whole 4x4x8 slice. The times are simulated.
256 devices in a mesh: param: 32 (over z, x), task: 8 (over y, core).
Axes of the slice: x: 4, y: 4, z: 8, core: 2. Of those that a mesh axis runs over, the one named last changes fastest.
Arguments:
- task_ids: int32 [1024], P('task'), may hold values from 0 to 2047
- task_table: bfloat16 [2048, 256], P('param'), may hold values from -12 to 12
- enc_in: bfloat16 [256, 512], replicated, may hold values from -0.375 to 0.375
- enc_out: bfloat16 [512, 256], replicated, may hold values from -0.25 to 0.25
- generator: bfloat16 [256, 8, 114688], P(None, None, ('param', 'task')), may hold values from -6 to 6
- gain: bfloat16 [8, 114688], P(None, ('param', 'task')), may hold values from 0.099609375 to 1.8984375
Outputs:
- adapters: bfloat16 [1024, 8, 114688], P(None, None, ('param', 'task'))
Inputs may be any that keep to these rules, and one draw needn't show every extreme that they name: `task_ids`: each id names a row of task_table.
All inputs are finite; a program needn't handle non-finite values.
Results may differ from a plain program's by a relative error of at most 0.00055.
The roundings to bfloat16 on the way count: a program that leaves them out, or rounds other values in their place, can miss the bound.
Values may be sent and summed in bfloat16 or wider, within the bound.
No kernel may reach another device: no remote copies, remote signals or barrier semaphores. Data moves between devices by JAX's collectives and lax.ppermute only.
A program may use at most 64 MiB of HBM per device.

v0:
```python
import jax
import jax.numpy as jnp
from jax import lax
from jax.sharding import Mesh
from jax.sharding import PartitionSpec as P

D = 3584
RANK = 32
PARAM = ("param_0", "param_1")
TASK = ("task_0", "task_1")
PARAM_TASK = ("param_0", "param_1", "task_0", "task_1")
EPSILON = 1e-06


def laid_out(tiles, dim):
    lengths = list(tiles.shape[1:])
    lengths[dim] *= tiles.shape[0]
    return jnp.moveaxis(tiles, 0, dim).reshape(lengths)


def copy_for_each(x, axis):
    copies = jnp.broadcast_to(x, (lax.axis_size(axis), *x.shape))
    return lax.all_to_all(copies, axis, split_axis=0, concat_axis=0, tiled=True)


def gathered_copies(x, axis, dim):
    return laid_out(copy_for_each(x, axis), dim)


def over_copies(x, axis):
    return copy_for_each(x, axis).sum(axis=0)


def by_axis(x, axes):
    far, near = axes
    return over_copies(over_copies(x, near), far)


def select_rows(wanted, table_part):
    labels = lax.broadcasted_iota(jnp.int32, (1, table_part.shape[0]), 1)
    one_hot = (wanted[:, None] == labels).astype(jnp.bfloat16)
    return jnp.dot(one_hot, table_part, preferred_element_type=jnp.float32)


def look_up(wanted, task_table):
    whole_table = gathered_copies(task_table, PARAM, 0)
    found = select_rows(wanted, whole_table).astype(jnp.bfloat16)
    return found


def encode(raw_rows, enc_in, enc_out):
    inner_act = jax.nn.gelu(jnp.dot(raw_rows, enc_in, preferred_element_type=jnp.float32)).astype(
        jnp.bfloat16
    )
    mixed_sum = raw_rows.astype(jnp.float32) + jnp.dot(
        inner_act, enc_out, preferred_element_type=jnp.float32
    )
    return mixed_sum.astype(jnp.bfloat16)


def on_device(task_ids, task_table, enc_in, enc_out, generator, gain):
    groups = generator.shape[1]
    columns = generator.shape[2]
    flat_weights = generator.reshape(generator.shape[0], groups * columns)
    every_id = lax.all_gather(task_ids, TASK, axis=0, tiled=True)
    embedded = encode(look_up(every_id, task_table), enc_in, enc_out)
    generated = jnp.dot(embedded, flat_weights, preferred_element_type=jnp.float32)
    generated = generated.reshape(generated.shape[0], groups, columns)
    squares = jnp.sum(generated * generated, axis=2)
    totals = by_axis(squares, ("param_0", ("param_1", "task_0", "task_1")))
    inverse = lax.rsqrt(totals / (D * RANK) + EPSILON)
    scaled = generated * inverse[:, :, None] * gain.astype(jnp.float32)[None, :, :]
    return scaled.astype(jnp.bfloat16)


def solution(mesh):
    torus = Mesh(mesh.devices.reshape(8, 4, 4, 2), ("param_0", "param_1", "task_0", "task_1"))
    return jax.shard_map(
        on_device,
        mesh=torus,
        in_specs=(
            P(TASK),
            P(PARAM, None),
            P(),
            P(),
            P(None, None, PARAM_TASK),
            P(None, PARAM_TASK),
        ),
        out_specs=P(None, None, PARAM_TASK),
        check_vma=False,
    )
```

profile of v0, /device:TPU:1, one launch (start us, length us, event | category | flops | bytes accessed | tf_op | source)
XLA Modules:
  0.0 105.5 jit_solution(1677882748042664104)
XLA Ops:
  0.0 0.0 copy-start
  0.0 0.0 copy-start.2
  0.0 2.0 %broadcast_in_dim.12 = bf16[32,64,256]{2,1,0:T(8,128)(2,1)} broadcast(bf16[64,256]{1,0:T(8,128)(2,1)} %param.7), dimensions={1,2} | broadcast | bytes 1081344 | tf_op jit(solution)/shard_map/broadcast_in_dim | solution.py:22
  2.0 11.9 %all-to-all-start = ((bf16[32,64,256]{2,1,0:T(8,128)(2,1)}), bf16[32,64,256]{2,1,0:T(8,128)(2,1)S(1)}, u32[]{:S(2)}, u32[]{:S(2)}) async-start(bf16[32,64,256]{2,1,0:T(8,128)(2,1)} %broadcast_in_dim.12), calls=%async_computation | async-start | bytes 2097152 | tf_op jit(solution)/shard_map/all_to_all | solution.py:23
  13.9 0.0 copy-done.2
  13.9 11.6 %all-gather = s32[8,1,128]{2,1,0:T(1,128)S(1)} all-gather(s32[1,1,128]{2,1,0:T(1,128)S(1)} %bitcast.21), channel_id=1, replica_groups=mesh['param_0'=8,'param_1'=4,'task_0'=4,'task_1'=2] {'task_0','task_1'}, dimensions={0}, use_global_device_ids=true | all-gather | bytes 4608 | tf_op jit(solution)/shard_map/all_gather | solution.py:65
  25.5 14.6 %all-to-all-done = bf16[32,64,256]{2,1,0:T(8,128)(2,1)S(1)} async-done(((bf16[32,64,256]{2,1,0:T(8,128)(2,1)}), bf16[32,64,256]{2,1,0:T(8,128)(2,1)S(1)}, u32[]{:S(2)}, u32[]{:S(2)}) %all-to-all-start) | async-done | bytes 1048608 | tf_op jit(solution)/shard_map/all_to_all | solution.py:23
  40.1 0.0 copy-start.3
  40.1 0.0 copy-start.4
  40.1 2.3 %fusion.15 = bf16[1024,256]{1,0:T(8,128)(2,1)} fusion(bf16[2048,256]{1,0:T(8,128)(2,1)S(1)} %bitcast.19, s32[1024]{0:T(1024)S(1)} %bitcast.20), kind=kOutput, calls=%fused_computation.19 | convolution fusion | flops 1076101120 | bytes 1576960 | tf_op jit(solution)/shard_map/dot_general | solution.py:42
  42.4 0.0 copy-done.3
  42.4 0.0 copy-done.4
  42.4 2.2 %fusion.16 = bf16[1024,256,1]{1,0,2:T(8,128)(2,1)S(1)} fusion(bf16[512,256]{1,0:T(8,128)(2,1)S(1)} %copy-done.3, bf16[1024,256]{1,0:T(8,128)(2,1)} %fusion.15, bf16[256,512]{1,0:T(8,128)(2,1)S(1)} %copy-done.4), kind=kOutput, calls=%fused_computation.20 | convolution fusion | flops 542375936 | bytes 1572864 | tf_op jit(solution)/shard_map/dot_general | solution.py:55
  44.6 0.0 copy-done
  44.6 7.3 %multiply_reduce_fusion = (f32[1024,8]{0,1:T(8,128)S(1)}, f32[1024,8,448]{0,2,1:T(8,128)}) fusion(bf16[1024,256,1]{1,0,2:T(8,128)(2,1)S(1)} %fusion.16, bf16[256,8,448]{0,2,1:T(8,128)(2,1)S(1)} %copy-done), kind=kOutput, calls=%fused_computation.1 | convolution fusion | flops 1886380032 | bytes 17072128 | tf_op jit(solution)/shard_map/dot_general | solution.py:67
  51.9 0.1 broadcast_in_dim.13
  52.0 0.0 copy-start.1
  52.1 26.9 %all_to_all.15 = f32[32,1024,8]{1,2,0:T(8,128)S(1)} all-to-all(f32[32,1024,8]{1,2,0:T(8,128)S(1)} %broadcast_in_dim.13), channel_id=1, replica_groups=mesh['param_0'=8,'param_1'=4,'task_0'=4,'task_1'=2] {'param_1','task_0',..., dimensions={0} | all-to-all | bytes 2097152 | tf_op jit(solution)/shard_map/all_to_all | solution.py:23
  79.0 0.1 reduce_sum.28
  79.0 0.7 broadcast_in_dim.14
  79.7 3.4 %all-to-all-start.2 = ((f32[8,1024,8]{1,2,0:T(8,128)}), f32[8,1024,8]{1,2,0:T(8,128)S(1)}, u32[]{:S(2)}, u32[]{:S(2)}) async-start(f32[8,1024,8]{1,2,0:T(8,128)} %broadcast_in_dim.14), calls=%async_computation.2 | async-start | bytes 524288 | tf_op jit(solution)/shard_map/all_to_all | solution.py:23
  83.2 0.0 copy-done.1
  83.2 12.3 %all-to-all-done.2 = f32[8,1024,8]{1,2,0:T(8,128)S(1)} async-done(((f32[8,1024,8]{1,2,0:T(8,128)}), f32[8,1024,8]{1,2,0:T(8,128)S(1)}, u32[]{:S(2)}, u32[]{:S(2)}) %all-to-all-start.2) | async-done | bytes 262176 | tf_op jit(solution)/shard_map/all_to_all | solution.py:23
  95.5 10.0 %multiply_convert_fusion = bf16[1024,8,448]{0,2,1:T(8,128)(2,1)} fusion(f32[1024,8,448]{0,2,1:T(8,128)} %get-tuple-element.6, f32[8,448]{1,0:T(8,128)S(1)} %convert_element_type.23, f32[1024,8]{0,1:T(8,128)S(1)} %add_rsqrt_fusion), kind=kLoop, calls=%fused_computation | loop fusion | flops 11010048 | bytes 22067200 | tf_op jit(solution)/shard_map/convert_element_type | solution.py:73
  (3 shorter events, 0.0 us)
Async XLA Ops:
  0.0 44.6 %copy-start = (bf16[256,8,448]{0,2,1:T(8,128)(2,1)S(1)}, bf16[256,8,448]{0,2,1:T(8,128)(2,1)}, u32[]{:S(2)}) copy-start(bf16[256,8,448]{0,2,1:T(8,128)(2,1)} %param.10) | copy-start | bytes 5505028
  0.0 13.9 %copy-start.2 = (s32[128]{0:T(128)S(1)}, s32[128]{0:T(128)}, u32[]{:S(2)}) copy-start(s32[128]{0:T(128)} %param.6) | copy-start | bytes 1540
  2.0 38.1 %all-to-all-start = ((bf16[32,64,256]{2,1,0:T(8,128)(2,1)}), bf16[32,64,256]{2,1,0:T(8,128)(2,1)S(1)}, u32[]{:S(2)}, u32[]{:S(2)}) async-start(bf16[32,64,256]{2,1,0:T(8,128)(2,1)} %broadcast_in_dim.12), calls=%async_computation | async-start | bytes 2097152 | tf_op jit(solution)/shard_map/all_to_all | solution.py:23
  40.1 2.3 %copy-start.3 = (bf16[512,256]{1,0:T(8,128)(2,1)S(1)}, bf16[512,256]{1,0:T(8,128)(2,1)}, u32[]{:S(2)}) copy-start(bf16[512,256]{1,0:T(8,128)(2,1)} %param.9) | copy-start | bytes 786436
  40.1 2.3 %copy-start.4 = (bf16[256,512]{1,0:T(8,128)(2,1)S(1)}, bf16[256,512]{1,0:T(8,128)(2,1)}, u32[]{:S(2)}) copy-start(bf16[256,512]{1,0:T(8,128)(2,1)} %param.8) | copy-start | bytes 786436
  52.0 31.1 %copy-start.1 = (bf16[8,448]{1,0:T(8,128)(2,1)S(1)}, bf16[8,448]{1,0:T(8,128)(2,1)}, u32[]{:S(2)}) copy-start(bf16[8,448]{1,0:T(8,128)(2,1)} %param.11) | copy-start | bytes 21508
  79.7 15.7 %all-to-all-start.2 = ((f32[8,1024,8]{1,2,0:T(8,128)}), f32[8,1024,8]{1,2,0:T(8,128)S(1)}, u32[]{:S(2)}, u32[]{:S(2)}) async-start(f32[8,1024,8]{1,2,0:T(8,128)} %broadcast_in_dim.14), calls=%async_computation.2 | async-start | bytes 524288 | tf_op jit(solution)/shard_map/all_to_all | solution.py:23
where the time goes:
time: 106 us
  blocking collectives  38.5 us (36%)
  waiting for transfers between devices  26.9 us (25%)
  starting transfers between devices  15.3 us (14%)
  matrix products  11.9 us (11%)
  other arithmetic  10.1 us (10%)
  local copies, waits for them, and re-layouts  2.84 us (3%)
    all_to_all x1, blocking collectives, copy_for_each(): return lax.all_to_all(copies, axis, split_axis=0, concat_axis=0, tiled=True)  26.9 us
    all_to_all x2, waiting for transfers between devices, copy_for_each(): return lax.all_to_all(copies, axis, split_axis=0, concat_axis=0, tiled=True)  26.9 us
    all_to_all x2, starting transfers between devices, copy_for_each(): return lax.all_to_all(copies, axis, split_axis=0, concat_axis=0, tiled=True)  15.3 us
    all_gather x1, blocking collectives, on_device(): every_id = lax.all_gather(task_ids, TASK, axis=0, tiled=True)  11.6 us
    convert_element_type x1, other arithmetic, on_device(): return scaled.astype(jnp.bfloat16)  10 us
    dot_general x1, matrix products, on_device(): jnp.dot(embedded, flat_weights, preferred_element_type=jnp.float32)  7.32 us
    broadcast_in_dim x3, local copies, waits for them, and re-layouts, copy_for_each(): copies = jnp.broadcast_to(x, (lax.axis_size(axis), *x.shape))  2.82 us
    dot_general x1, matrix products, select_rows(): return jnp.dot(one_hot, table_part, preferred_element_type=jnp.float32)  2.3 us
  transfers between devices with their start and end apart: 2, of which 2 were waited for; matrix products, arithmetic and copies ran while one was open for 0% of the time, Pallas kernels for 0%

commit v1 on v0

--- a/solution.py
+++ b/solution.py
@@ -62,7 +62,9 @@
     groups = generator.shape[1]
     columns = generator.shape[2]
     flat_weights = generator.reshape(generator.shape[0], groups * columns)
-    every_id = lax.all_gather(task_ids, TASK, axis=0, tiled=True)
+    every_id = jnp.concatenate(
+        lax.all_to_all(jnp.stack([task_ids] * lax.axis_size(TASK)), TASK, 0, 0), axis=0
+    )
     embedded = encode(look_up(every_id, task_table), enc_in, enc_out)
     generated = jnp.dot(embedded, flat_weights, preferred_element_type=jnp.float32)
     generated = generated.reshape(generated.shape[0], groups, columns)

time: 106 us -> 111 us (1.047)
  blocking collectives: 38.5 us -> 72.2 us
  waiting for transfers between devices: 26.9 us -> 12.3 us
  starting transfers between devices: 15.3 us -> 3.41 us
  matrix products: 11.9 us -> 9.81 us
    all_to_all x1 -> x2, blocking collectives: 26.9 us -> 61.9 us  [copy_for_each(): return lax.all_to_all(copies, axis, split_axis=0, concat_axis=0, tiled=True)]
    all_to_all x2 -> x1, waiting for transfers between devices: 26.9 us -> 12.3 us  [copy_for_each(): return lax.all_to_all(copies, axis, split_axis=0, concat_axis=0, tiled=True)]
    all_to_all x2 -> x1, starting transfers between devices: 15.3 us -> 3.41 us  [copy_for_each(): return lax.all_to_all(copies, axis, split_axis=0, concat_axis=0, tiled=True)]
    all_gather x1 -> x0, blocking collectives: 11.6 us -> none  [on_device(): every_id = lax.all_gather(task_ids, TASK, axis=0, tiled=True)]
    all_to_all x0 -> x1, blocking collectives: none -> 10.3 us  [on_device(): lax.all_to_all(jnp.stack([task_ids] * lax.axis_size(TASK)), TASK, 0, 0)]
    dot_general x1, matrix products: 2.23 us -> 0.97 us  [encode(): jnp.dot(inner_act, enc_out, preferred_element_type=jnp.float32)]
    broadcast_in_dim x3, local copies, waits for them, and re-layouts: 2.82 us -> 1.69 us  [copy_for_each(): copies = jnp.broadcast_to(x, (lax.axis_size(axis), *x.shape))]
  transfers between devices with their start and end apart: 2 -> 1, of which waited for: 2 -> 1; matrix products, arithmetic and copies ran while one was open for 0% -> 0% of each run, Pallas kernels for 0% -> 0%
where the time goes in v1:
time: 111 us; the launch traced here: 110 us
  blocking collectives  72.2 us (65%)
  waiting for transfers between devices  12.3 us (11%)
  other arithmetic  9.82 us (9%)
  matrix products  9.81 us (9%)
  starting transfers between devices  3.41 us (3%)
  local copies, waits for them, and re-layouts  2.5 us (2%)
    all_to_all x2, blocking collectives, copy_for_each(): return lax.all_to_all(copies, axis, split_axis=0, concat_axis=0, tiled=True)  61.9 us
    all_to_all x1, waiting for transfers between devices, copy_for_each(): return lax.all_to_all(copies, axis, split_axis=0, concat_axis=0, tiled=True)  12.3 us
    all_to_all x1, blocking collectives, on_device(): lax.all_to_all(jnp.stack([task_ids] * lax.axis_size(TASK)), TASK, 0, 0)  10.3 us
    convert_element_type x1, other arithmetic, on_device(): return scaled.astype(jnp.bfloat16)  9.71 us
    dot_general x1, matrix products, on_device(): jnp.dot(embedded, flat_weights, preferred_element_type=jnp.float32)  7.34 us
    all_to_all x1, starting transfers between devices, copy_for_each(): return lax.all_to_all(copies, axis, split_axis=0, concat_axis=0, tiled=True)  3.41 us
  transfers between devices with their start and end apart: 1, of which 1 were waited for; matrix products, arithmetic and copies ran while one was open for 0% of the time, Pallas kernels for 0%

profile of v1, /device:TPU:1, one launch (start us, length us, event | category | flops | bytes accessed | tf_op | source)
XLA Modules:
  0.0 110.2 jit_solution(14558475522826182364)
XLA Ops:
  0.0 0.0 copy-start
  0.0 0.8 stack.2
  0.8 10.3 %all_to_all.21 = s32[8,1,128]{2,1,0:T(1,128)S(1)} all-to-all(s32[8,1,128]{2,1,0:T(1,128)S(1)} %stack.2), channel_id=1, replica_groups=mesh['param_0'=8,'param_1'=4,'task_0'=4,'task_1'=2] {'task_0','task_1'}, dimensions={0} | all-to-all | bytes 8192 | tf_op jit(solution)/shard_map/all_to_all | solution.py:66
  11.1 0.9 broadcast_in_dim.11
  12.0 37.0 %all_to_all.22 = bf16[32,64,256]{2,1,0:T(8,128)(2,1)S(1)} all-to-all(bf16[32,64,256]{2,1,0:T(8,128)(2,1)S(1)} %broadcast_in_dim.11), channel_id=1, replica_groups=mesh['param_0'=8,'param_1'=4,'task_0'=4,'task_1'=2] {'param_0','param_1'}, dimensions={0} | all-to-all | bytes 2097152 | tf_op jit(solution)/shard_map/all_to_all | solution.py:23
  49.0 0.0 copy-start.2
  49.0 0.0 copy-start.3
  49.0 1.5 %fusion.15 = bf16[1024,256]{1,0:T(8,128)(2,1)S(1)} fusion(bf16[2048,256]{1,0:T(8,128)(2,1)S(1)} %bitcast.18, s32[1024]{0:T(1024)S(1)} %bitcast.19), kind=kOutput, calls=%fused_computation.19 | convolution fusion | flops 1076101120 | bytes 1576960 | tf_op jit(solution)/shard_map/dot_general | solution.py:42
  50.6 0.0 copy-done.2
  50.6 0.0 copy-done.3
  50.6 1.0 fusion.16
  51.6 0.0 copy-done
  51.6 7.3 %multiply_reduce_fusion = (f32[1024,8]{0,1:T(8,128)S(1)}, f32[1024,8,448]{0,2,1:T(8,128)}) fusion(bf16[1024,256,1]{1,0,2:T(8,128)(2,1)S(1)} %fusion.16, bf16[256,8,448]{0,2,1:T(8,128)(2,1)S(1)} %copy-done), kind=kOutput, calls=%fused_computation.1 | convolution fusion | flops 1886380032 | bytes 17072128 | tf_op jit(solution)/shard_map/dot_general | solution.py:69
  58.9 0.1 broadcast_in_dim.12
  59.0 0.0 copy-start.1
  59.0 24.9 %all_to_all.23 = f32[32,1024,8]{1,2,0:T(8,128)S(1)} all-to-all(f32[32,1024,8]{1,2,0:T(8,128)S(1)} %broadcast_in_dim.12), channel_id=1, replica_groups=mesh['param_0'=8,'param_1'=4,'task_0'=4,'task_1'=2] {'param_1','task_0',..., dimensions={0} | all-to-all | bytes 2097152 | tf_op jit(solution)/shard_map/all_to_all | solution.py:23
  83.9 0.1 reduce_sum.28
  84.0 0.7 broadcast_in_dim.13
  84.7 3.4 %all-to-all-start.3 = ((f32[8,1024,8]{1,2,0:T(8,128)}), f32[8,1024,8]{1,2,0:T(8,128)S(1)}, u32[]{:S(2)}, u32[]{:S(2)}) async-start(f32[8,1024,8]{1,2,0:T(8,128)} %broadcast_in_dim.13), calls=%async_computation.3 | async-start | bytes 524288 | tf_op jit(solution)/shard_map/all_to_all | solution.py:23
  88.1 0.0 copy-done.1
  88.1 12.3 %all-to-all-done.3 = f32[8,1024,8]{1,2,0:T(8,128)S(1)} async-done(((f32[8,1024,8]{1,2,0:T(8,128)}), f32[8,1024,8]{1,2,0:T(8,128)S(1)}, u32[]{:S(2)}, u32[]{:S(2)}) %all-to-all-start.3) | async-done | bytes 262176 | tf_op jit(solution)/shard_map/all_to_all | solution.py:23
  100.4 9.7 %multiply_convert_fusion = bf16[1024,8,448]{0,2,1:T(8,128)(2,1)} fusion(f32[1024,8,448]{0,2,1:T(8,128)} %get-tuple-element.6, f32[8,448]{1,0:T(8,128)S(1)} %convert_element_type.23, f32[1024,8]{0,1:T(8,128)S(1)} %add_rsqrt_fusion), kind=kLoop, calls=%fused_computation | loop fusion | flops 11010048 | bytes 22067200 | tf_op jit(solution)/shard_map/convert_element_type | solution.py:75
  (3 shorter events, 0.0 us)
Async XLA Ops:
  0.0 51.6 %copy-start = (bf16[256,8,448]{0,2,1:T(8,128)(2,1)S(1)}, bf16[256,8,448]{0,2,1:T(8,128)(2,1)}, u32[]{:S(2)}) copy-start(bf16[256,8,448]{0,2,1:T(8,128)(2,1)} %param.10) | copy-start | bytes 5505028
  49.0 1.5 %copy-start.2 = (bf16[512,256]{1,0:T(8,128)(2,1)S(1)}, bf16[512,256]{1,0:T(8,128)(2,1)}, u32[]{:S(2)}) copy-start(bf16[512,256]{1,0:T(8,128)(2,1)} %param.9) | copy-start | bytes 786436
  49.0 1.5 %copy-start.3 = (bf16[256,512]{1,0:T(8,128)(2,1)S(1)}, bf16[256,512]{1,0:T(8,128)(2,1)}, u32[]{:S(2)}) copy-start(bf16[256,512]{1,0:T(8,128)(2,1)} %param.8) | copy-start | bytes 786436
  59.0 29.1 %copy-start.1 = (bf16[8,448]{1,0:T(8,128)(2,1)S(1)}, bf16[8,448]{1,0:T(8,128)(2,1)}, u32[]{:S(2)}) copy-start(bf16[8,448]{1,0:T(8,128)(2,1)} %param.11) | copy-start | bytes 21508
  84.7 15.7 %all-to-all-start.3 = ((f32[8,1024,8]{1,2,0:T(8,128)}), f32[8,1024,8]{1,2,0:T(8,128)S(1)}, u32[]{:S(2)}, u32[]{:S(2)}) async-start(f32[8,1024,8]{1,2,0:T(8,128)} %broadcast_in_dim.13), calls=%async_computation.3 | async-start | bytes 524288 | tf_op jit(solution)/shard_map/all_to_all | solution.py:23
